TPU v7x, 32 devices: a whole 2x2x4 slice. The times are simulated.
32 devices in a mesh: row: 4 (over y, x), col: 8 (over z, core).
Axes of the slice: x: 2, y: 2, z: 4, core: 2. Of those that a mesh axis runs over, the one named last changes fastest.
Arguments:
- iterates: float32 [11, 1024], P(None, ('col', 'row')), may hold values from -6 to 6
- residuals: float32 [11, 1024], P(None, ('col', 'row')), may hold values from -3 to 3
- operator: float32 [16384, 1024], P('row', 'col'), may hold values from -0.1875 to 0.1875
- target: float32 [16384], replicated, may hold values from -6 to 6
- cone_id: int32 [16384], replicated, may hold values from 0 to 2047, never falling along the last dimension, each value on 1 to 16 neighbouring positions
Outputs:
- next_point: float32 [1024], P(('col', 'row'))
- projected: float32 [16384], P('row')
Inputs may be any that keep to these rules, and one draw needn't show every extreme that they name: cone_id never falls along the rows; each of the 2048 cones holds 1 to 16 consecutive rows.
All inputs are finite; a program needn't handle non-finite values.
Results may differ from a plain program's by a relative error of at most 0.0003.
Values sent between devices are 32-bit elements; how exact they have to be, the bound alone decides.
No kernel may reach another device: no remote copies, remote signals or barrier semaphores. Data moves between devices by JAX's collectives and lax.ppermute only.
A program may use at most 64 MiB of HBM per device.

v0:
```python
import math
import jax
import jax.numpy as jnp
from jax import lax
from jax.sharding import PartitionSpec as P

HIGH = lax.Precision.HIGHEST
RIM = 16


def with_halo(x, sides, width):
    for axis, dim in sides:
        devices, length = (lax.axis_size(axis), x.shape[dim])
        up = [(i, (i + 1) % devices) for i in range(devices - 1)]
        down = [(j, i) for i, j in up]
        last = lax.slice_in_dim(x, length - width, length, axis=dim)
        leading = lax.slice_in_dim(x, 0, width, axis=dim)
        before = lax.ppermute(last, axis, up)
        after = lax.ppermute(leading, axis, down)
        x = jnp.concatenate([before, x, after], axis=dim)
    return x


def solve_weights(gram, right_side):
    count = gram.shape[0]
    shifted = gram + 0.01 * (jnp.trace(gram) / count) * jnp.eye(count, dtype=jnp.float32)
    factor = jnp.linalg.cholesky(shifted)
    return jax.scipy.linalg.cho_solve((factor, True), right_side)


def window_cones(slack_ext, ids_ext, head_ext, length):
    shifts = range(1 - RIM, RIM)
    slack_win = jnp.stack([slack_ext[RIM + s : RIM + s + length] for s in shifts])
    ids_win = jnp.stack([ids_ext[RIM + s : RIM + s + length] for s in shifts])
    head_win = jnp.stack([head_ext[RIM + s : RIM + s + length] for s in shifts])
    own_ids = ids_ext[RIM : RIM + length]
    slack = slack_ext[RIM : RIM + length]
    head_own = head_ext[RIM : RIM + length]
    same = (ids_win == own_ids[None, :]).astype(jnp.float32)
    head_row = jnp.sum(same * head_win * slack_win, axis=0)
    tail_tot = jnp.sum(same * (1.0 - head_win) * slack_win * slack_win, axis=0)
    norm_row = jnp.sqrt(tail_tot)
    inside = norm_row <= head_row
    killed = norm_row <= -head_row
    safe_norm = jnp.where(norm_row > 0, norm_row, 1.0)
    middle = 0.5 * (head_row + norm_row)
    outside = jnp.where(head_own > 0, middle, middle * slack / safe_norm)
    return jnp.where(inside, slack, jnp.where(killed, 0.0, outside))


def body(iterates, residuals, operator, target, cone_id):
    row_count = lax.axis_size("row")
    col_count = lax.axis_size("col")
    row_block = operator.shape[0]
    local_len = iterates.shape[1]
    all_rows = row_block * row_count
    scale_back = math.sqrt(local_len * row_count * col_count / all_rows)
    row_index = lax.axis_index("row")
    row_offset = row_index * row_block
    delta_x = iterates[1:] - iterates[:-1]
    delta_f = residuals[1:] - residuals[:-1]
    last_f = residuals[-1]
    gram_local = jnp.dot(delta_f, delta_f.T, precision=HIGH)
    side_local = jnp.dot(delta_f, last_f, precision=HIGH)
    anchor = iterates[-1] + last_f
    step_dirs = delta_x + delta_f
    gram, right_side = lax.psum((gram_local, side_local), ("row", "col"))
    weights = solve_weights(gram, right_side)
    blended = anchor - jnp.dot(weights, step_dirs, precision=HIGH)
    columns = operator
    partial_value = jnp.zeros((row_block,), jnp.float32) + jnp.dot(
        columns, lax.all_gather(blended, "row", axis=0, tiled=True), precision=HIGH
    )
    image_own = lax.psum(partial_value, "col")
    head_all = jnp.concatenate(
        [jnp.ones((1,), jnp.float32), (cone_id[1:] != cone_id[:-1]).astype(jnp.float32)]
    )
    ids_pad = jnp.concatenate(
        [jnp.full((RIM,), -1, jnp.int32), cone_id, jnp.full((RIM,), -1, jnp.int32)]
    )
    head_pad = jnp.concatenate(
        [jnp.zeros((RIM,), jnp.float32), head_all, jnp.zeros((RIM,), jnp.float32)]
    )
    ids_ext = lax.dynamic_slice_in_dim(ids_pad, row_offset, row_block + 2 * RIM, 0)
    head_ext = lax.dynamic_slice_in_dim(head_pad, row_offset, row_block + 2 * RIM, 0)
    slack_own = lax.dynamic_slice_in_dim(target, row_offset, row_block, 0) - image_own
    slack_ext = with_halo(slack_own, (("row", 0),), RIM)
    slack_own = slack_ext[RIM : RIM + row_block]
    proj_own = window_cones(slack_ext, ids_ext, head_ext, row_block)
    correction = proj_own - slack_own
    columns = operator
    back = lax.psum_scatter(
        jnp.dot(correction, columns, precision=HIGH), "row", scatter_dimension=0, tiled=True
    )
    next_point = blended - scale_back * back
    return (next_point, proj_own)


def solution(mesh):
    return jax.shard_map(
        body,
        mesh=mesh,
        in_specs=(P(None, ("col", "row")), P(None, ("col", "row")), P("row", "col"), P(), P()),
        out_specs=(P(("col", "row")), P("row")),
        check_vma=False,
    )
```

profile of v0, /device:TPU:0, one launch (start us, length us, event | category | flops | bytes accessed | tf_op | source)
XLA Modules:
  0.0 124.1 jit_solution(8513609570144858646)
XLA Ops:
  0.6 0.0 copy-start
  0.6 0.0 copy-start.1
  0.7 1.0 convolution_bitcast_fusion.3
  1.7 1.0 fusion.48
  2.7 42.1 %all-reduce.2 = (f32[10,10]{0,1:T(8,128)S(1)}, f32[10]{0:T(128)S(1)}) all-reduce(f32[10,10]{0,1:T(8,128)S(1)} %fusion.48, f32[10]{0:T(128)S(1)} %convolution_bitcast_fusion.3), channel_id=1, replica_groups=mesh['row'=4,'col'=8] {'row','col'}, use_global_device_ids=true, to_apply=%region_0.0 | all-reduce | flops 110 | bytes 880 | tf_op jit(solution)/shard_map/psum | solution.py:67
  44.7 0.6 select_reduce_fusion.1
  46.0 0.1 copy.20
  46.1 0.9 cholesky.17
  47.0 0.1 copy.21
  47.1 0.1 select_reduce_fusion
  47.2 0.6 compare_reduce_fusion
  47.9 0.6 select_select_fusion
  48.5 0.1 copy.23
  48.6 0.8 custom-call.10
  49.4 0.1 convolution_bitcast_fusion.2
  49.5 0.1 convolution_bitcast_fusion.1
  49.7 1.4 %fusion.56 = (u32[1]{0:T(128)}, u32[1]{0:T(128)}) fusion(u32[32]{0:T(128)} %constant.89, u32[]{:T(128)S(6)} %add.52, u32[]{:T(128)S(6)} %add.49), kind=kLoop, calls=%fused_computation.136 | loop fusion | bytes 24
  51.7 0.9 fusion
  52.6 0.0 copy-start.2
  52.6 0.2 dynamic-update-slice.3
  52.9 0.3 copy-done.2
  53.1 9.7 %all-reduce = f32[128]{0:T(128)S(1)} all-reduce(f32[128]{0:T(128)S(1)} %dynamic-update-slice.3), channel_id=1, replica_groups=mesh['row'=4,'col'=8] {'row'}, use_global_device_ids=true, to_apply=%add | all-reduce | flops 128 | bytes 1024
  62.9 0.0 copy-done
  62.9 1.8 %fusion.43 = f32[1,4096]{1,0:T(1,128)S(1)} fusion(f32[4096,128]{1,0:T(8,128)S(1)} %copy-done, f32[128]{0:T(128)S(1)} %all-reduce), kind=kOutput, calls=%fused_computation.123 | convolution fusion | flops 6291456 | bytes 2114048 | tf_op jit(solution)/shard_map/dot_general | solution.py:71
  64.7 25.9 %psum.23 = f32[4096]{0:T(1024)S(1)} all-reduce(f32[4096]{0:T(1024)S(1)} %bitcast.210), channel_id=1, replica_groups=mesh['row'=4,'col'=8] {'col'}, use_global_device_ids=true, to_apply=%region_5.6 | all-reduce | flops 4096 | bytes 32768 | tf_op jit(solution)/shard_map/psum | solution.py:74
  90.6 0.7 dynamic-slice_subtract_fusion
  91.3 0.6 fusion.55
  91.9 1.3 %collective-permute-start.1 = (f32[16]{0:T(128)}, f32[16]{0:T(128)}, u32[]{:S(2)}, u32[]{:S(2)}) collective-permute-start(f32[16]{0:T(128)} %get-tuple-element.100), channel_id=1, source_target_pairs={{8,0},{16,8},{24,16},{9,1},{17,9},{25,17},{10,2},{18,10},{26,18},{... | collective-permute-start | bytes 200 | tf_op jit(solution)/shard_map/ppermute | solution.py:19
  93.2 5.1 %collective-permute-start = (f32[16]{0:T(128)}, f32[16]{0:T(128)}, u32[]{:S(2)}, u32[]{:S(2)}) collective-permute-start(f32[16]{0:T(128)} %get-tuple-element.101), channel_id=1, source_target_pairs={{0,8},{8,16},{16,24},{1,9},{9,17},{17,25},{2,10},{10,18},{18,26},{... | collective-permute-start | bytes 200 | tf_op jit(solution)/shard_map/ppermute | solution.py:18
  98.3 0.0 copy-done.1
  98.3 0.1 fusion.2
  98.4 0.1 concatenate.41
  98.5 0.1 concatenate.42
  98.6 0.8 fusion.54
  99.4 0.2 fusion.52
  99.6 0.3 fusion.51
  99.9 0.3 fusion.53
  100.8 0.8 stack.351
  101.5 1.6 %stack.319 = s32[31,4096]{1,0:T(8,128)S(1)} concatenate(s32[1,4096]{1,0:T(1,128)} %bitcast.224, s32[1,4096]{1,0:T(1,128)} %bitcast.223, s32[1,4096]{1,0:T(1,128)} %bitcast.222, s32[1,4096]{1,0:T(1,128)} %bitcast.221, s32[1,4096]{1,0:T(1,128)} %bitcast.220, s32[1,4096]{1,0:T(1,128)} %bitcast.219, s32[1,4096]{1,0:T(1,128)} %bitcast.218, s32[1,4096]{1,0:T(1,128)} %bitcast.217, ...), dimensions={0} | concatenate | bytes 1015808 | tf_op jit(solution)/shard_map/stack | solution.py:34
  103.1 0.0 collective-permute-done.1
  103.1 1.1 pad_maximum_fusion
  104.2 1.0 fusion.3
  105.2 0.0 collective-permute-done
  105.2 1.0 fusion.17
  106.2 1.7 %pad_maximum_fusion.1 = (f32[4096]{0:T(1024)S(1)}, f32[4096]{0:T(1024)}, f32[4096]{0:T(1024)}, f32[4096]{0:T(1024)}, f32[4096]{0:T(1024)}, /*index=5*/f32[4096]{...) fusion(f32[4096]{0:T(1024)S(1)} %dynamic-slice_subtract_fusion, f32[16]{0:T(128)} %collective-permute-done), kind=kLoop, calls=%fused_computation.102 | loop fusion | flops 36864 | bytes 163904 | tf_op jit(solution)/shard_map/concatenate | solution.py:20
  108.0 4.1 %stack.383 = f32[31,4096]{1,0:T(8,128)} concatenate(f32[1,4096]{1,0:T(1,128)} %bitcast.202, f32[1,4096]{1,0:T(1,128)} %bitcast.203, f32[1,4096]{1,0:T(1,128)} %bitcast.204, f32[1,4096]{1,0:T(1,128)} %bitcast.205, f32[1,4096]{1,0:T(1,128)} %bitcast.206, f32[1,4096]{1,0:T(1,128)} %bitcast.207, f32[1,4096]{1,0:T(1,128)} %bitcast.208, f32[1,4096]{1,0:T(1,128)} %bitcast.209, ...), dimensions={0} | concatenate | bytes 1015808 | tf_op jit(solution)/shard_map/stack | solution.py:33
  112.1 0.0 copy-start.3
  112.1 1.3 %fusion.1 = (f32[4096]{0:T(1024)S(1)}, f32[4096]{0:T(1024)S(1)}) fusion(f32[31,4096]{1,0:T(8,128)} %stack.383, f32[31,4096]{1,0:T(8,128)S(1)} %stack.351, s32[31,4096]{1,0:T(8,128)S(1)} %stack.319, s32[4096]{0:T(1024)S(1)} %get-tuple-element.54), kind=kLoop, calls=%fused_computation.7 | loop fusion | flops 1134592 | bytes 1572864 | tf_op jit(solution)/shard_map/reduce_sum | solution.py:41
  113.4 0.6 fusion.49
  114.0 1.1 convolution_bitcast_fusion.4
  115.1 8.4 %all-reduce.1 = f32[128]{0:T(128)S(1)} all-reduce(f32[128]{0:T(128)S(1)} %convolution_bitcast_fusion.4), channel_id=2, replica_groups=mesh['row'=4,'col'=8] {'row'}, use_global_device_ids=true, to_apply=%region_8.9.clone | all-reduce | flops 128 | bytes 1024
  123.5 0.0 copy-done.3
  123.5 0.6 fusion.42
  (5 shorter events, 0.0 us)
Async XLA Ops:
  0.6 62.2 %copy-start = (f32[4096,128]{1,0:T(8,128)S(1)}, f32[4096,128]{1,0:T(8,128)}, u32[]{:S(2)}) copy-start(f32[4096,128]{1,0:T(8,128)} %param.7) | copy-start | bytes 6291460
  0.6 97.7 %copy-start.1 = (s32[16384]{0:T(1024)S(1)}, s32[16384]{0:T(1024)}, u32[]{:S(2)}) copy-start(s32[16384]{0:T(1024)} %param.9) | copy-start | bytes 196612
  52.6 0.5 copy-start.2
  91.9 11.2 %collective-permute-start.1 = (f32[16]{0:T(128)}, f32[16]{0:T(128)}, u32[]{:S(2)}, u32[]{:S(2)}) collective-permute-start(f32[16]{0:T(128)} %get-tuple-element.100), channel_id=1, source_target_pairs={{8,0},{16,8},{24,16},{9,1},{17,9},{25,17},{10,2},{18,10},{26,18},{... | collective-permute-start | bytes 200 | tf_op jit(solution)/shard_map/ppermute | solution.py:19
  93.2 12.0 %collective-permute-start = (f32[16]{0:T(128)}, f32[16]{0:T(128)}, u32[]{:S(2)}, u32[]{:S(2)}) collective-permute-start(f32[16]{0:T(128)} %get-tuple-element.101), channel_id=1, source_target_pairs={{0,8},{8,16},{16,24},{1,9},{9,17},{17,25},{2,10},{10,18},{18,26},{... | collective-permute-start | bytes 200 | tf_op jit(solution)/shard_map/ppermute | solution.py:18
  112.1 11.4 %copy-start.3 = (f32[32]{0:T(128)S(1)}, f32[32]{0:T(128)}, u32[]{:S(2)}) copy-start(f32[32]{0:T(128)} %copy-done.2) | copy-start | bytes 388
where the time goes:
time: 125 us; the launch traced here: 124 us
  blocking collectives  86.1 us (69%)
  other arithmetic  11.8 us (9%)
  local copies, waits for them, and re-layouts  10.9 us (9%)
  starting transfers between devices  6.42 us (5%)
  matrix products  6.11 us (5%)
  between operations  2.75 us (2%)
    psum x1, blocking collectives, body(): gram, right_side = lax.psum((gram_local, side_local), ('row', 'col'))  42.1 us
    psum x1, blocking collectives, body(): image_own = lax.psum(partial_value, 'col')  25.9 us
    unnamed x2, blocking collectives  18.1 us
    ppermute x1, starting transfers between devices, with_halo(): before = lax.ppermute(last, axis, up)  5.14 us
    concatenate x4, other arithmetic, with_halo(): x = jnp.concatenate([before, x, after], axis=dim)  4.81 us
    another operation x1, local copies, waits for them, and re-layouts, window_cones(): slack_win = jnp.stack([slack_ext[RIM + s:RIM + s + length] for s in shifts])  4.14 us
  transfers between devices with their start and end apart: 2, of which 0 were waited for; matrix products, arithmetic and copies ran while one was open for 5% of the time, Pallas kernels for 0%

commit v1 on v0

--- a/solution.py
+++ b/solution.py
@@ -71,7 +71,16 @@
     partial_value = jnp.zeros((row_block,), jnp.float32) + jnp.dot(
         columns, lax.all_gather(blended, "row", axis=0, tiled=True), precision=HIGH
     )
-    image_own = lax.psum(partial_value, "col")
+
+    def lead_the_knots(z):
+        out_arr = z
+        k_all = lax.axis_size("col")
+        for src_i in [u for u in (1, 2, 4, 8, 16) if u < k_all]:
+            b_now = lax.ppermute(out_arr, "col", perm=[(p, p ^ src_i) for p in range(k_all)])
+            out_arr = out_arr + b_now
+        return out_arr
+
+    image_own = lead_the_knots(partial_value)
     head_all = jnp.concatenate(
         [jnp.ones((1,), jnp.float32), (cone_id[1:] != cone_id[:-1]).astype(jnp.float32)]
     )

time: 125 us -> 104 us (0.83)
  blocking collectives: 86.1 us -> 62.4 us
  starting transfers between devices: 6.42 us -> 9.7 us
  other arithmetic: 11.8 us -> 8.68 us
  waiting for transfers between devices: 0.01 us -> 2.83 us
    psum x1 -> x0, blocking collectives: 25.9 us -> none  [body(): image_own = lax.psum(partial_value, 'col')]
    ppermute x0 -> x3, starting transfers between devices: none -> 3.87 us  [lead_the_knots(): lax.ppermute(out_arr, 'col', perm=[(p, p ^ src_i) for p in range(k_all)])]
    concatenate x4, other arithmetic: 4.81 us -> 1.04 us  [with_halo(): x = jnp.concatenate([before, x, after], axis=dim)]
    unnamed x2, blocking collectives: 18.1 us -> 20.3 us
    ppermute x0 -> x3, waiting for transfers between devices: none -> 1.77 us  [lead_the_knots(): lax.ppermute(out_arr, 'col', perm=[(p, p ^ src_i) for p in range(k_all)])]
  transfers between devices with their start and end apart: 2 -> 5, of which waited for: 0 -> 3; matrix products, arithmetic and copies ran while one was open for 5% -> 4% of each run, Pallas kernels for 0% -> 0%
where the time goes in v1:
time: 104 us; the launch traced here: 103 us
  blocking collectives  62.4 us (60%)
  local copies, waits for them, and re-layouts  10.5 us (10%)
  starting transfers between devices  9.7 us (9%)
  other arithmetic  8.68 us (8%)
  matrix products  6.11 us (6%)
  waiting for transfers between devices  2.83 us (3%)
  between operations  2.7 us (3%)
    psum x1, blocking collectives, body(): gram, right_side = lax.psum((gram_local, side_local), ('row', 'col'))  42.1 us
    unnamed x2, blocking collectives  20.3 us
    ppermute x1, starting transfers between devices, with_halo(): before = lax.ppermute(last, axis, up)  4.55 us
    another operation x1, local copies, waits for them, and re-layouts, window_cones(): slack_win = jnp.stack([slack_ext[RIM + s:RIM + s + length] for s in shifts])  4.14 us
    ppermute x3, starting transfers between devices, lead_the_knots(): lax.ppermute(out_arr, 'col', perm=[(p, p ^ src_i) for p in range(k_all)])  3.87 us
  transfers between devices with their start and end apart: 5, of which 3 were waited for; matrix products, arithmetic and copies ran while one was open for 4% of the time, Pallas kernels for 0%

profile of v1, /device:TPU:0, one launch (start us, length us, event | category | flops | bytes accessed | tf_op | source)
XLA Modules:
  0.0 103.0 jit_solution(9117856282770932098)
XLA Ops:
  0.6 0.0 copy-start
  0.6 0.0 copy-start.1
  0.7 1.0 convolution_bitcast_fusion.3
  1.7 1.0 fusion.48
  2.7 42.1 %all-reduce.2 = (f32[10,10]{0,1:T(8,128)S(1)}, f32[10]{0:T(128)S(1)}) all-reduce(f32[10,10]{0,1:T(8,128)S(1)} %fusion.48, f32[10]{0:T(128)S(1)} %convolution_bitcast_fusion.3), channel_id=1, replica_groups=mesh['row'=4,'col'=8] {'row','col'}, use_global_device_ids=true, to_apply=%region_0.0 | all-reduce | flops 110 | bytes 880 | tf_op jit(solution)/shard_map/psum | solution.py:67
  44.7 0.6 select_reduce_fusion.1
  46.0 0.1 copy.20
  46.1 0.9 cholesky.17
  47.0 0.1 copy.21
  47.1 0.1 select_reduce_fusion
  47.2 0.6 compare_reduce_fusion
  47.9 0.6 select_select_fusion
  48.5 0.1 copy.23
  48.6 0.8 custom-call.10
  49.4 0.1 convolution_bitcast_fusion.2
  49.6 0.1 convolution_bitcast_fusion.1
  49.7 1.3 %fusion.56 = (u32[1]{0:T(128)}, u32[1]{0:T(128)}) fusion(u32[32]{0:T(128)} %constant.89, u32[]{:T(128)S(6)} %add.62, u32[]{:T(128)S(6)} %add.59), kind=kLoop, calls=%fused_computation.136 | loop fusion | bytes 24
  51.7 0.9 fusion
  52.6 0.0 copy-start.2
  52.6 0.5 copy-done.2
  53.1 0.2 dynamic-update-slice.3
  53.3 9.7 %all-reduce = f32[128]{0:T(128)S(1)} all-reduce(f32[128]{0:T(128)S(1)} %dynamic-update-slice.3), channel_id=1, replica_groups=mesh['row'=4,'col'=8] {'row'}, use_global_device_ids=true, to_apply=%add | all-reduce | flops 128 | bytes 1024
  63.0 0.0 copy-done
  63.0 1.8 %fusion.43 = f32[1,4096]{1,0:T(1,128)S(1)} fusion(f32[4096,128]{1,0:T(8,128)S(1)} %copy-done, f32[128]{0:T(128)S(1)} %all-reduce), kind=kOutput, calls=%fused_computation.123 | convolution fusion | flops 6291456 | bytes 2114048 | tf_op jit(solution)/shard_map/dot_general | solution.py:71
  64.8 0.0 collective-permute-start
  64.9 0.0 copy-done.1
  64.9 0.1 fusion.2
  65.0 0.1 concatenate.41
  65.1 0.1 concatenate.42
  65.2 0.3 fusion.51
  65.5 0.3 fusion.53
  65.8 0.3 collective-permute-done
  66.1 1.5 %collective-permute-start.1 = (f32[4096]{0:T(1024)S(1)}, f32[4096]{0:T(1024)S(1)}, u32[]{:S(2)}, u32[]{:S(2)}) collective-permute-start(f32[4096]{0:T(1024)S(1)} %add.55), channel_id=1, source_target_pairs={{0,2},{1,3},{2,0},{3,1},{4,6},{5,7},{6,4},{7,5},{8,10},{9,11},{10,... | collective-permute-start | bytes 49160 | tf_op jit(solution)/shard_map/ppermute | solution.py:79
  67.6 0.8 fusion.54
  68.3 1.5 %collective-permute-done.1 = f32[4096]{0:T(1024)S(1)} collective-permute-done((f32[4096]{0:T(1024)S(1)}, f32[4096]{0:T(1024)S(1)}, u32[]{:S(2)}, u32[]{:S(2)}) %collective-permute-start.1) | collective-permute-done | bytes 16416 | tf_op jit(solution)/shard_map/ppermute | solution.py:79
  69.8 0.6 add.56
  70.4 2.3 %collective-permute-start.2 = (f32[4096]{0:T(1024)}, f32[4096]{0:T(1024)}, u32[]{:S(2)}, u32[]{:S(2)}) collective-permute-start(f32[4096]{0:T(1024)} %add.56), channel_id=1, source_target_pairs={{0,4},{1,5},{2,6},{3,7},{4,0},{5,1},{6,2},{7,3},{8,12},{9,13},{10,... | collective-permute-start | bytes 49160 | tf_op jit(solution)/shard_map/ppermute | solution.py:79
  72.7 0.2 fusion.52
  73.5 0.8 stack.351
  74.2 1.6 %stack.319 = s32[31,4096]{1,0:T(8,128)S(1)} concatenate(s32[1,4096]{1,0:T(1,128)} %bitcast.225, s32[1,4096]{1,0:T(1,128)} %bitcast.224, s32[1,4096]{1,0:T(1,128)} %bitcast.223, s32[1,4096]{1,0:T(1,128)} %bitcast.222, s32[1,4096]{1,0:T(1,128)} %bitcast.221, s32[1,4096]{1,0:T(1,128)} %bitcast.220, s32[1,4096]{1,0:T(1,128)} %bitcast.219, s32[1,4096]{1,0:T(1,128)S(1)} %bitcast.218, ...), dimensions={0} | concatenate | bytes 1015808 | tf_op jit(solution)/shard_map/stack | solution.py:34
  75.8 0.0 collective-permute-done.2
  75.8 0.8 add_subtract_fusion
  76.6 0.1 fusion.55
  76.6 1.3 %collective-permute-start.4 = (f32[16]{0:T(128)S(1)}, f32[16]{0:T(128)S(1)}, u32[]{:S(2)}, u32[]{:S(2)}) collective-permute-start(f32[16]{0:T(128)S(1)} %get-tuple-element.100), channel_id=1, source_target_pairs={{8,0},{16,8},{24,16},{9,1},{17,9},{25,17},{10,2},{18,10},{26,18},{... | collective-permute-start | bytes 200 | tf_op jit(solution)/shard_map/ppermute | solution.py:19
  77.9 4.5 %collective-permute-start.3 = (f32[16]{0:T(128)S(1)}, f32[16]{0:T(128)S(1)}, u32[]{:S(2)}, u32[]{:S(2)}) collective-permute-start(f32[16]{0:T(128)S(1)} %get-tuple-element.101), channel_id=1, source_target_pairs={{0,8},{8,16},{16,24},{1,9},{9,17},{17,25},{2,10},{10,18},{18,26},{... | collective-permute-start | bytes 200 | tf_op jit(solution)/shard_map/ppermute | solution.py:18
  82.5 0.0 collective-permute-done.4
  82.5 0.1 pad_maximum_fusion
  82.6 0.1 fusion.3
  82.7 1.0 %collective-permute-done.3 = f32[16]{0:T(128)S(1)} collective-permute-done((f32[16]{0:T(128)S(1)}, f32[16]{0:T(128)S(1)}, u32[]{:S(2)}, u32[]{:S(2)}) %collective-permute-start.3) | collective-permute-done | bytes 96 | tf_op jit(solution)/shard_map/ppermute | solution.py:18
  83.8 0.1 fusion.17
  83.9 0.7 pad_maximum_fusion.1
  84.6 4.1 %stack.383 = f32[31,4096]{1,0:T(8,128)} concatenate(f32[1,4096]{1,0:T(1,128)} %bitcast.204, f32[1,4096]{1,0:T(1,128)} %bitcast.205, f32[1,4096]{1,0:T(1,128)} %bitcast.206, f32[1,4096]{1,0:T(1,128)} %bitcast.207, f32[1,4096]{1,0:T(1,128)} %bitcast.208, f32[1,4096]{1,0:T(1,128)} %bitcast.209, f32[1,4096]{1,0:T(1,128)} %bitcast.210, f32[1,4096]{1,0:T(1,128)} %bitcast.211, ...), dimensions={0} | concatenate | bytes 1015808 | tf_op jit(solution)/shard_map/stack | solution.py:33
  88.7 0.0 copy-start.3
  88.7 1.3 %fusion.1 = (f32[4096]{0:T(1024)S(1)}, f32[4096]{0:T(1024)S(1)}) fusion(f32[31,4096]{1,0:T(8,128)} %stack.383, f32[31,4096]{1,0:T(8,128)S(1)} %stack.351, s32[31,4096]{1,0:T(8,128)S(1)} %stack.319, s32[4096]{0:T(1024)S(1)} %get-tuple-element.54), kind=kLoop, calls=%fused_computation.7 | loop fusion | flops 1134592 | bytes 1572864 | tf_op jit(solution)/shard_map/reduce_sum | solution.py:41
  90.0 0.6 fusion.49
  90.6 1.1 %convolution_bitcast_fusion.4 = f32[128]{0:T(128)S(1)} fusion(f32[4096,1]{0,1:T(1,128)S(1)} %bitcast.212, f32[4096,128]{1,0:T(8,128)S(1)} %copy-done), kind=kOutput, calls=%fused_computation.5 | convolution fusion | flops 6291456 | bytes 2114048 | tf_op jit(solution)/shard_map/dot_general | solution.py:102
  91.8 10.6 %all-reduce.1 = f32[128]{0:T(128)S(1)} all-reduce(f32[128]{0:T(128)S(1)} %convolution_bitcast_fusion.4), channel_id=2, replica_groups=mesh['row'=4,'col'=8] {'row'}, use_global_device_ids=true, to_apply=%region_7.8.clone | all-reduce | flops 128 | bytes 1024
  102.4 0.0 copy-done.3
  102.4 0.6 fusion.42
  (6 shorter events, 0.0 us)
Async XLA Ops:
  0.6 62.4 %copy-start = (f32[4096,128]{1,0:T(8,128)S(1)}, f32[4096,128]{1,0:T(8,128)}, u32[]{:S(2)}) copy-start(f32[4096,128]{1,0:T(8,128)} %param.7) | copy-start | bytes 6291460
  0.6 64.2 %copy-start.1 = (s32[16384]{0:T(1024)S(1)}, s32[16384]{0:T(1024)}, u32[]{:S(2)}) copy-start(s32[16384]{0:T(1024)} %param.9) | copy-start | bytes 196612
  52.6 0.5 copy-start.2
  64.8 1.2 %collective-permute-start = (f32[4096]{0:T(1024)S(1)}, f32[4096]{0:T(1024)S(1)}, u32[]{:S(2)}, u32[]{:S(2)}) collective-permute-start(f32[4096]{0:T(1024)S(1)} %bitcast.180), channel_id=1, source_target_pairs={{0,1},{1,0},{2,3},{3,2},{4,5},{5,4},{6,7},{7,6},{8,9},{9,8},{10,11... | collective-permute-start | bytes 49160 | tf_op jit(solution)/shard_map/ppermute | solution.py:79
  66.1 3.7 %collective-permute-start.1 = (f32[4096]{0:T(1024)S(1)}, f32[4096]{0:T(1024)S(1)}, u32[]{:S(2)}, u32[]{:S(2)}) collective-permute-start(f32[4096]{0:T(1024)S(1)} %add.55), channel_id=1, source_target_pairs={{0,2},{1,3},{2,0},{3,1},{4,6},{5,7},{6,4},{7,5},{8,10},{9,11},{10,... | collective-permute-start | bytes 49160 | tf_op jit(solution)/shard_map/ppermute | solution.py:79
  70.4 5.4 %collective-permute-start.2 = (f32[4096]{0:T(1024)}, f32[4096]{0:T(1024)}, u32[]{:S(2)}, u32[]{:S(2)}) collective-permute-start(f32[4096]{0:T(1024)} %add.56), channel_id=1, source_target_pairs={{0,4},{1,5},{2,6},{3,7},{4,0},{5,1},{6,2},{7,3},{8,12},{9,13},{10,... | collective-permute-start | bytes 49160 | tf_op jit(solution)/shard_map/ppermute | solution.py:79
  76.6 5.8 %collective-permute-start.4 = (f32[16]{0:T(128)S(1)}, f32[16]{0:T(128)S(1)}, u32[]{:S(2)}, u32[]{:S(2)}) collective-permute-start(f32[16]{0:T(128)S(1)} %get-tuple-element.100), channel_id=1, source_target_pairs={{8,0},{16,8},{24,16},{9,1},{17,9},{25,17},{10,2},{18,10},{26,18},{... | collective-permute-start | bytes 200 | tf_op jit(solution)/shard_map/ppermute | solution.py:19
  77.9 5.8 %collective-permute-start.3 = (f32[16]{0:T(128)S(1)}, f32[16]{0:T(128)S(1)}, u32[]{:S(2)}, u32[]{:S(2)}) collective-permute-start(f32[16]{0:T(128)S(1)} %get-tuple-element.101), channel_id=1, source_target_pairs={{0,8},{8,16},{16,24},{1,9},{9,17},{17,25},{2,10},{10,18},{18,26},{... | collective-permute-start | bytes 200 | tf_op jit(solution)/shard_map/ppermute | solution.py:18
  88.7 13.6 %copy-start.3 = (f32[32]{0:T(128)S(1)}, f32[32]{0:T(128)}, u32[]{:S(2)}) copy-start(f32[32]{0:T(128)} %copy-done.2) | copy-start | bytes 388
